TPU v7x, 32 devices: a whole 2x2x4 slice. The times are simulated.
32 devices in a mesh: bank: 4 (over y, x), zero: 8 (over z, core).
Axes of the slice: x: 2, y: 2, z: 4, core: 2. Of those that a mesh axis runs over, the one named last changes fastest.
Arguments:
- train_gate: float32 [64, 2048, 1024], P('bank', 'zero'), may hold values from -0.1875 to 0.1875
- train_up: float32 [64, 2048, 1024], P('bank', 'zero'), may hold values from -0.1875 to 0.1875
- train_down: float32 [64, 1024, 2048], P('bank', None, 'zero'), may hold values from -0.25 to 0.25
- router_weight: float32 [2048, 64], P('zero', 'bank'), may hold values from -0.125 to 0.125
- router_gain: float32 [2048], P('zero'), may hold values from 0.25 to 1.75
Outputs:
- ready_gate: bfloat16 [64, 2048, 1024], P('bank', None, 'zero')
- ready_up: bfloat16 [64, 2048, 1024], P('bank', None, 'zero')
- ready_down: bfloat16 [64, 1024, 2048], P('bank', 'zero')
- scale_gate: float32 [64, 1024], P('bank', 'zero')
- scale_up: float32 [64, 1024], P('bank', 'zero')
- scale_down: float32 [64, 1024], P('bank', 'zero')
- serve_router: bfloat16 [2048, 64], replicated
All inputs are finite; a program needn't handle non-finite values.
Results may differ from a plain program's by a relative error of at most 0.001.
Values may be sent and summed in bfloat16 or wider, within the bound.
A program may use at most 192 MiB of HBM per device.

v0:
```python
import jax
import jax.numpy as jnp
from jax import lax
from jax.sharding import PartitionSpec as P


def on_device(train_gate, train_up, train_down, router_weight, router_gain):
    total_gate, total_up, total_down = lax.psum(
        (
            jnp.sum(train_gate * train_gate, axis=1),
            jnp.sum(train_up * train_up, axis=1),
            jnp.sum(train_down * train_down, axis=2),
        ),
        "zero",
    )
    scale_gate = jnp.sqrt(total_gate)
    scale_up = jnp.sqrt(total_up)
    scale_down = jnp.sqrt(total_down)
    narrow_gate, narrow_up, narrow_down = (
        (train_gate / jnp.expand_dims(scale_gate, 1)).astype(jnp.bfloat16),
        (train_up / jnp.expand_dims(scale_up, 1)).astype(jnp.bfloat16),
        (train_down / jnp.expand_dims(scale_down, 2)).astype(jnp.bfloat16),
    )
    ready_gate, ready_up = (
        lax.all_to_all(narrow_gate, "zero", split_axis=2, concat_axis=1, tiled=True),
        lax.all_to_all(narrow_up, "zero", split_axis=2, concat_axis=1, tiled=True),
    )
    ready_down = lax.all_to_all(narrow_down, "zero", split_axis=1, concat_axis=2, tiled=True)
    scale_gate = lax.dynamic_slice_in_dim(
        scale_gate, lax.axis_index("zero") * ready_gate.shape[2], ready_gate.shape[2], axis=1
    )
    scale_up = lax.dynamic_slice_in_dim(
        scale_up, lax.axis_index("zero") * ready_up.shape[2], ready_up.shape[2], axis=1
    )
    scale_down = lax.dynamic_slice_in_dim(
        scale_down, lax.axis_index("zero") * ready_down.shape[1], ready_down.shape[1], axis=1
    )
    part_router = (router_weight * router_gain[:, None]).astype(jnp.bfloat16)
    row_router = lax.all_gather(part_router, "zero", axis=0, tiled=True)
    serve_router = lax.all_gather(row_router, "bank", axis=1, tiled=True)
    return (ready_gate, ready_up, ready_down, scale_gate, scale_up, scale_down, serve_router)


def solution(mesh):
    return jax.shard_map(
        on_device,
        mesh=mesh,
        in_specs=(
            P("bank", "zero", None),
            P("bank", "zero", None),
            P("bank", None, "zero"),
            P("zero", "bank"),
            P("zero"),
        ),
        out_specs=(
            P("bank", None, "zero"),
            P("bank", None, "zero"),
            P("bank", "zero", None),
            P("bank", "zero"),
            P("bank", "zero"),
            P("bank", "zero"),
            P(),
        ),
        check_vma=False,
    )
```

profile of v0, /device:TPU:0, one launch (start us, length us, event | category | flops | bytes accessed | tf_op | source)
XLA Modules:
  0.0 737.8 jit_solution(13230997140834230480)
XLA Ops:
  7.2 0.0 all-reduce.3.cloned.1.call-start
  7.2 8.6 %multiply_reduce_fusion = f32[16,1024]{1,0:T(8,128)} fusion(f32[16,1024,256]{2,1,0:T(8,128)} %param.7), kind=kLoop, calls=%fused_computation.2 | loop fusion | flops 8372224 | bytes 16842752 | tf_op jit(solution)/shard_map/reduce_sum | solution.py:12
  15.8 12.6 %multiply_reduce_fusion.1 = (f32[16,1024]{1,0:T(8,128)}, f32[16,1024]{1,0:T(8,128)}) fusion(f32[16,256,1024]{2,1,0:T(8,128)} %param.6, f32[16,256,1024]{2,1,0:T(8,128)} %param.5), kind=kLoop, calls=%fused_computation.4 | loop fusion | flops 16744448 | bytes 33685504 | tf_op jit(solution)/shard_map/reduce_sum | solution.py:11
  28.4 0.0 all-reduce.3.cloned.1.call-update
  28.4 17.6 %copy.19 = f32[16,256,1024]{1,0,2:T(8,128)} copy(f32[16,256,1024]{2,1,0:T(8,128)} %param.6) | data formatting | bytes 33554432 | tf_op args[1]
  46.1 40.7 %all-reduce.3.cloned.1.call-done = (f32[16,1024]{1,0:T(8,128)}, f32[16,1024]{1,0:T(8,128)}, f32[16,1024]{1,0:T(8,128)}) async-done(((f32[16,1024]{1,0:T(8,128)}, f32[16,1024]{1,0:T(8,128)}, f32[16,1024]{1,0:T(8,128)}), (f32[16,1024]{1,0:T(8,128)}, f32[16,1024]{1,0:T(8,128)}, f32[16,1024]{1,0:T(8,128)})) %all-reduce.3.cloned.1.call-update) | async-done | bytes 196624 | tf_op jit(solution)/shard_map/psum | solution.py:8
  86.8 0.9 sqrt.10
  87.6 0.2 copy.18
  87.8 9.6 %divide_convert_fusion = bf16[16,256,1024]{1,0,2:T(8,128)(2,1)} fusion(f32[16,256,1024]{1,0,2:T(8,128)} %copy.19, f32[16,1024]{0,1:T(8,128)S(1)} %copy.18), kind=kLoop, calls=%fused_computation.3 | loop fusion | flops 8388608 | bytes 25231360 | tf_op jit(solution)/shard_map/convert_element_type | solution.py:21
  97.5 4.9 all-to-all-start.1
  102.4 0.0 copy-start.1
  102.4 17.6 %copy.16 = f32[16,256,1024]{1,0,2:T(8,128)} copy(f32[16,256,1024]{2,1,0:T(8,128)} %param.5) | data formatting | bytes 33554432 | tf_op args[0]
  120.1 0.0 copy-done.1
  120.1 0.2 copy.15
  120.3 0.0 copy-start
  120.3 9.7 %divide_convert_fusion.1 = bf16[16,256,1024]{1,0,2:T(8,128)(2,1)} fusion(f32[16,256,1024]{1,0,2:T(8,128)} %copy.16, f32[16,1024]{0,1:T(8,128)S(1)} %copy.15), kind=kLoop, calls=%fused_computation.5 | loop fusion | flops 8388608 | bytes 25231360 | tf_op jit(solution)/shard_map/convert_element_type | solution.py:20
  130.0 156.3 %all-to-all-done.1 = bf16[16,256,1024]{1,0,2:T(8,128)(2,1)} async-done(((bf16[16,256,1024]{1,0,2:T(8,128)(2,1)}), bf16[16,256,1024]{1,0,2:T(8,128)(2,1)}, u32[]{:S(2)}, u32[]{:S(2)}) %all-to-all-start.1) | async-done | bytes 8388640 | tf_op jit(solution)/shard_map/all_to_all | solution.py:26
  286.3 4.9 all-to-all-start
  291.2 0.0 copy-done
  291.3 0.2 copy.21
  291.5 0.0 copy-start.2
  291.5 0.0 copy-start.3
  291.5 16.6 %fusion = bf16[16,1024,256]{2,0,1:T(8,128)(2,1)} fusion(f32[16,1024,256]{2,1,0:T(8,128)} %param.7, f32[16,1024]{0,1:T(8,128)S(1)} %copy.21), kind=kLoop, calls=%fused_computation.1 | loop fusion | flops 8388608 | bytes 25231360 | tf_op jit(solution)/shard_map/convert_element_type | solution.py:22
  308.1 167.0 %all-to-all-done = bf16[16,256,1024]{1,0,2:T(8,128)(2,1)} async-done(((bf16[16,256,1024]{1,0,2:T(8,128)(2,1)}), bf16[16,256,1024]{1,0,2:T(8,128)(2,1)}, u32[]{:S(2)}, u32[]{:S(2)}) %all-to-all-start) | async-done | bytes 8388640 | tf_op jit(solution)/shard_map/all_to_all | solution.py:25
  475.1 5.0 all-to-all-start.2
  480.1 0.0 copy-done.2
  480.1 0.0 copy-done.3
  480.2 189.9 %all_gather.6 = bf16[2048,16]{0,1:T(8,128)(2,1)S(1)} all-gather(bf16[256,16]{0,1:T(8,128)(2,1)S(1)} %multiply_convert_fusion), channel_id=1, replica_groups=mesh['bank'=4,'zero'=8] {'zero'}, dimensions={0}, use_global_device_ids=true | all-gather | bytes 73728 | tf_op jit(solution)/shard_map/all_gather | solution.py:39
  670.0 9.1 %all_gather.7 = bf16[2048,64]{0,1:T(8,128)(2,1)S(1)} all-gather(bf16[2048,16]{0,1:T(8,128)(2,1)S(1)} %all_gather.6), channel_id=1, replica_groups=mesh['bank'=4,'zero'=8] {'bank'}, dimensions={1}, use_global_device_ids=true | all-gather | bytes 327680 | tf_op jit(solution)/shard_map/all_gather | solution.py:40
  679.1 0.6 constant_dynamic-slice_fusion
  679.7 0.6 constant_dynamic-slice_fusion.1
  680.3 0.6 constant_dynamic-slice_fusion.2
  680.9 12.3 %copy.20 = bf16[16,8,256,128]{3,2,1,0:T(8,128)(2,1)} copy(bf16[16,8,256,128]{2,0,3,1:T(8,128)(2,1)} %bitcast.4) | data formatting | bytes 16777216 | tf_op jit(solution)/shard_map/all_to_all | solution.py:26
  693.2 12.3 %copy.17 = bf16[16,8,256,128]{3,2,1,0:T(8,128)(2,1)} copy(bf16[16,8,256,128]{2,0,3,1:T(8,128)(2,1)} %bitcast.1) | data formatting | bytes 16777216 | tf_op jit(solution)/shard_map/all_to_all | solution.py:25
  705.5 0.0 all-to-all-done.2
  705.5 11.4 %copy.23 = bf16[16,128,8,256]{3,2,1,0:T(8,128)(2,1)} copy(bf16[16,128,8,256]{3,0,1,2:T(8,128)(2,1)} %bitcast.7) | data formatting | bytes 16777216 | tf_op jit(solution)/shard_map/all_to_all | solution.py:28
  716.9 13.4 %all_to_all.50 = bf16[16,128,2048]{2,1,0:T(8,128)(2,1)} reshape(bf16[16,128,8,256]{3,2,1,0:T(8,128)(2,1)} %copy.23) | data formatting | bytes 16777216 | tf_op jit(solution)/shard_map/all_to_all | solution.py:28
  730.3 0.7 copy.31
  (3 shorter events, 0.0 us)
Async XLA Ops:
  7.2 79.6 %all-reduce.3.cloned.1.call-start = ((), (), s32[]{:S(2)}) async-start(), calls=%async_computation.3 | async-start | bytes 393216 | tf_op jit(solution)/shard_map/psum | solution.py:8
  97.5 188.8 %all-to-all-start.1 = ((bf16[16,256,1024]{1,0,2:T(8,128)(2,1)}), bf16[16,256,1024]{1,0,2:T(8,128)(2,1)}, u32[]{:S(2)}, u32[]{:S(2)}) async-start(bf16[16,256,1024]{1,0,2:T(8,128)(2,1)} %divide_convert_fusion), calls=%async_computation.1 | async-start | bytes 16777216 | tf_op jit(solution)/shard_map/all_to_all | solution.py:26
  102.4 17.6 %copy-start.1 = (f32[16,1024]{1,0:T(8,128)S(1)}, f32[16,1024]{1,0:T(8,128)}, u32[]{:S(2)}) copy-start(f32[16,1024]{1,0:T(8,128)} %get-tuple-element.7) | copy-start | bytes 196612
  120.3 170.9 %copy-start = (f32[16,1024]{1,0:T(8,128)S(1)}, f32[16,1024]{1,0:T(8,128)}, u32[]{:S(2)}) copy-start(f32[16,1024]{1,0:T(8,128)} %get-tuple-element.9) | copy-start | bytes 196612
  286.3 188.8 %all-to-all-start = ((bf16[16,256,1024]{1,0,2:T(8,128)(2,1)}), bf16[16,256,1024]{1,0,2:T(8,128)(2,1)}, u32[]{:S(2)}, u32[]{:S(2)}) async-start(bf16[16,256,1024]{1,0,2:T(8,128)(2,1)} %divide_convert_fusion.1), calls=%async_computation | async-start | bytes 16777216 | tf_op jit(solution)/shard_map/all_to_all | solution.py:25
  291.5 188.6 %copy-start.2 = (f32[256,16]{0,1:T(8,128)S(1)}, f32[256,16]{0,1:T(8,128)}, u32[]{:S(2)}) copy-start(f32[256,16]{0,1:T(8,128)} %param.8) | copy-start | bytes 49156
  291.5 188.6 %copy-start.3 = (f32[256]{0:T(256)S(1)}, f32[256]{0:T(256)}, u32[]{:S(2)}) copy-start(f32[256]{0:T(256)} %param.9) | copy-start | bytes 3076
  475.1 230.4 %all-to-all-start.2 = ((bf16[16,1024,256]{2,0,1:T(8,128)(2,1)}), bf16[16,1024,256]{2,0,1:T(8,128)(2,1)}, u32[]{:S(2)}, u32[]{:S(2)}) async-start(bf16[16,1024,256]{2,0,1:T(8,128)(2,1)} %fusion), calls=%async_computation.2 | async-start | bytes 16777216 | tf_op jit(solution)/shard_map/all_to_all | solution.py:28
Sparse Core Ops, SparseCore 0:
  28.6 58.1 all-reduce.2
where the time goes:
time: 740 us; the launch traced here: 738 us
  waiting for transfers between devices  364 us (49%)
  blocking collectives  199 us (27%)
  local copies, waits for them, and re-layouts  88.6 us (12%)
  other arithmetic  57.2 us (8%)
  starting transfers between devices  14.9 us (2%)
  between operations  14.2 us (2%)
    all_gather x1, blocking collectives, on_device(): row_router = lax.all_gather(part_router, 'zero', axis=0, tiled=True)  190 us
    all_to_all x1, waiting for transfers between devices, on_device(): lax.all_to_all(narrow_gate, 'zero', split_axis=2, concat_axis=1, tiled=True)  167 us
    all_to_all x1, waiting for transfers between devices, on_device(): lax.all_to_all(narrow_up, 'zero', split_axis=2, concat_axis=1, tiled=True)  156 us
    psum x1, waiting for transfers between devices, on_device(): lax.psum((jnp.sum(train_gate * train_gate, axis=1), jnp.sum(train_up * tr...  40.7 us
    unnamed x11, local copies, waits for them, and re-layouts  36 us
    all_to_all x2, local copies, waits for them, and re-layouts, on_device(): lax.all_to_all(narrow_down, 'zero', split_axis=1, concat_axis=2, tiled=True)  24.8 us
    convert_element_type x1, other arithmetic, on_device(): (train_down / jnp.expand_dims(scale_down, 2)).astype(jnp.bfloat16)  16.6 us
  transfers between devices with their start and end apart: 4, of which 3 were waited for; matrix products, arithmetic and copies ran while one was open for 12% of the time, Pallas kernels for 0%

commit v1 on v0

--- a/solution.py
+++ b/solution.py
@@ -5,6 +5,19 @@
 
 
 def on_device(train_gate, train_up, train_down, router_weight, router_gain):
+
+    def _refer_pools(u_in):
+        front = jnp.concatenate(
+            lax.all_to_all(
+                jnp.stack([u_in] * lax.axis_size("zero"), 0),
+                axis_name="zero",
+                split_axis=0,
+                concat_axis=0,
+            ),
+            0,
+        )
+        return front
+
     total_gate, total_up, total_down = lax.psum(
         (
             jnp.sum(train_gate * train_gate, axis=1),
@@ -36,7 +49,7 @@
         scale_down, lax.axis_index("zero") * ready_down.shape[1], ready_down.shape[1], axis=1
     )
     part_router = (router_weight * router_gain[:, None]).astype(jnp.bfloat16)
-    row_router = lax.all_gather(part_router, "zero", axis=0, tiled=True)
+    row_router = _refer_pools(part_router)
     serve_router = lax.all_gather(row_router, "bank", axis=1, tiled=True)
     return (ready_gate, ready_up, ready_down, scale_gate, scale_up, scale_down, serve_router)
 

time: 740 us -> 698 us (0.943)
  blocking collectives: 199 us -> 9.11 us
  waiting for transfers between devices: 364 us -> 505 us
    all_gather x1 -> x0, blocking collectives: 190 us -> none  [on_device(): row_router = lax.all_gather(part_router, 'zero', axis=0, tiled=True)]
    all_to_all x1, waiting for transfers between devices: 0.01 us -> 148 us  [on_device(): lax.all_to_all(narrow_down, 'zero', split_axis=1, concat_axis=2, tiled=True)]
  transfers between devices with their start and end apart: 4 -> 5, of which waited for: 3 -> 4; matrix products, arithmetic and copies ran while one was open for 12% -> 14% of each run, Pallas kernels for 0% -> 0%
where the time goes in v1:
time: 698 us; the launch traced here: 696 us
  waiting for transfers between devices  505 us (72%)
  local copies, waits for them, and re-layouts  89.2 us (13%)
  other arithmetic  57.2 us (8%)
  starting transfers between devices  21.3 us (3%)
  between operations  14.2 us (2%)
  blocking collectives  9.11 us (1%)
    all_to_all x1, waiting for transfers between devices, on_device(): lax.all_to_all(narrow_gate, 'zero', split_axis=2, concat_axis=1, tiled=True)  167 us
    all_to_all x1, waiting for transfers between devices, on_device(): lax.all_to_all(narrow_up, 'zero', split_axis=2, concat_axis=1, tiled=True)  156 us
    all_to_all x1, waiting for transfers between devices, on_device(): lax.all_to_all(narrow_down, 'zero', split_axis=1, concat_axis=2, tiled=True)  148 us
    unnamed x11, local copies, waits for them, and re-layouts  36 us
    psum x1, waiting for transfers between devices, on_device(): lax.psum((jnp.sum(train_gate * train_gate, axis=1), jnp.sum(train_up * tr...  33.8 us
    all_to_all x2, local copies, waits for them, and re-layouts, on_device(): lax.all_to_all(narrow_down, 'zero', split_axis=1, concat_axis=2, tiled=True)  24.8 us
    convert_element_type x1, other arithmetic, on_device(): (train_down / jnp.expand_dims(scale_down, 2)).astype(jnp.bfloat16)  16.6 us
  transfers between devices with their start and end apart: 5, of which 4 were waited for; matrix products, arithmetic and copies ran while one was open for 14% of the time, Pallas kernels for 0%

profile of v1, /device:TPU:0, one launch (start us, length us, event | category | flops | bytes accessed | tf_op | source)
XLA Modules:
  0.0 696.5 jit_solution(6480954519635393990)
XLA Ops:
  7.2 0.0 all-reduce.3.cloned.1.call-start
  7.2 8.6 %multiply_reduce_fusion = f32[16,1024]{1,0:T(8,128)} fusion(f32[16,1024,256]{2,1,0:T(8,128)} %param.7), kind=kLoop, calls=%fused_computation.2 | loop fusion | flops 8372224 | bytes 16842752 | tf_op jit(solution)/shard_map/reduce_sum | solution.py:25
  15.8 0.0 copy-start.2
  15.8 0.0 copy-start.3
  15.9 12.6 %multiply_reduce_fusion.1 = (f32[16,1024]{1,0:T(8,128)}, f32[16,1024]{1,0:T(8,128)}) fusion(f32[16,256,1024]{2,1,0:T(8,128)} %param.6, f32[16,256,1024]{2,1,0:T(8,128)} %param.5), kind=kLoop, calls=%fused_computation.4 | loop fusion | flops 16744448 | bytes 33685504 | tf_op jit(solution)/shard_map/reduce_sum | solution.py:24
  28.4 0.0 all-reduce.3.cloned.1.call-update
  28.5 0.0 copy-done.2
  28.5 0.0 copy-done.3
  28.5 0.6 stack.2
  29.1 6.4 all-to-all-start.3
  35.5 17.6 %copy.28 = f32[16,256,1024]{1,0,2:T(8,128)} copy(f32[16,256,1024]{2,1,0:T(8,128)} %param.6) | data formatting | bytes 33554432 | tf_op args[1]
  53.1 33.8 %all-reduce.3.cloned.1.call-done = (f32[16,1024]{1,0:T(8,128)}, f32[16,1024]{1,0:T(8,128)}, f32[16,1024]{1,0:T(8,128)}) async-done(((f32[16,1024]{1,0:T(8,128)}, f32[16,1024]{1,0:T(8,128)}, f32[16,1024]{1,0:T(8,128)}), (f32[16,1024]{1,0:T(8,128)}, f32[16,1024]{1,0:T(8,128)}, f32[16,1024]{1,0:T(8,128)})) %all-reduce.3.cloned.1.call-update) | async-done | bytes 196624 | tf_op jit(solution)/shard_map/psum | solution.py:21
  86.9 0.9 sqrt.10
  87.8 0.2 copy.27
  88.0 9.6 %divide_convert_fusion = bf16[16,256,1024]{1,0,2:T(8,128)(2,1)} fusion(f32[16,256,1024]{1,0,2:T(8,128)} %copy.28, f32[16,1024]{0,1:T(8,128)S(1)} %copy.27), kind=kLoop, calls=%fused_computation.3 | loop fusion | flops 8388608 | bytes 25231360 | tf_op jit(solution)/shard_map/convert_element_type | solution.py:34
  97.6 0.0 all-to-all-done.3
  97.6 5.0 all-to-all-start.1
  102.6 0.0 copy-start.1
  102.6 17.6 %copy.25 = f32[16,256,1024]{1,0,2:T(8,128)} copy(f32[16,256,1024]{2,1,0:T(8,128)} %param.5) | data formatting | bytes 33554432 | tf_op args[0]
  120.2 0.0 copy-done.1
  120.2 0.2 copy.24
  120.4 0.0 copy-start
  120.4 9.7 %divide_convert_fusion.1 = bf16[16,256,1024]{1,0,2:T(8,128)(2,1)} fusion(f32[16,256,1024]{1,0,2:T(8,128)} %copy.25, f32[16,1024]{0,1:T(8,128)S(1)} %copy.24), kind=kLoop, calls=%fused_computation.5 | loop fusion | flops 8388608 | bytes 25231360 | tf_op jit(solution)/shard_map/convert_element_type | solution.py:33
  130.1 156.3 %all-to-all-done.1 = bf16[16,256,1024]{1,0,2:T(8,128)(2,1)} async-done(((bf16[16,256,1024]{1,0,2:T(8,128)(2,1)}), bf16[16,256,1024]{1,0,2:T(8,128)(2,1)}, u32[]{:S(2)}, u32[]{:S(2)}) %all-to-all-start.1) | async-done | bytes 8388640 | tf_op jit(solution)/shard_map/all_to_all | solution.py:39
  286.4 4.9 all-to-all-start
  291.4 0.0 copy-done
  291.4 0.2 copy.30
  291.6 16.6 %fusion = bf16[16,1024,256]{2,0,1:T(8,128)(2,1)} fusion(f32[16,1024,256]{2,1,0:T(8,128)} %param.7, f32[16,1024]{0,1:T(8,128)S(1)} %copy.30), kind=kLoop, calls=%fused_computation.1 | loop fusion | flops 8388608 | bytes 25231360 | tf_op jit(solution)/shard_map/convert_element_type | solution.py:35
  308.3 167.0 %all-to-all-done = bf16[16,256,1024]{1,0,2:T(8,128)(2,1)} async-done(((bf16[16,256,1024]{1,0,2:T(8,128)(2,1)}), bf16[16,256,1024]{1,0,2:T(8,128)(2,1)}, u32[]{:S(2)}, u32[]{:S(2)}) %all-to-all-start) | async-done | bytes 8388640 | tf_op jit(solution)/shard_map/all_to_all | solution.py:38
  475.3 5.0 all-to-all-start.2
  480.3 0.6 constant_dynamic-slice_fusion
  480.9 0.6 constant_dynamic-slice_fusion.1
  481.5 0.6 constant_dynamic-slice_fusion.2
  482.1 9.1 %all_gather.3 = bf16[2048,64]{0,1:T(8,128)(2,1)S(1)} all-gather(bf16[2048,16]{0,1:T(8,128)(2,1)S(1)} %bitcast.17), channel_id=1, replica_groups=mesh['bank'=4,'zero'=8] {'bank'}, dimensions={1}, use_global_device_ids=true | all-gather | bytes 327680 | tf_op jit(solution)/shard_map/all_gather | solution.py:53
  491.2 12.3 %copy.29 = bf16[16,8,256,128]{3,2,1,0:T(8,128)(2,1)} copy(bf16[16,8,256,128]{2,0,3,1:T(8,128)(2,1)} %bitcast.4) | data formatting | bytes 16777216 | tf_op jit(solution)/shard_map/all_to_all | solution.py:39
  503.5 12.3 %copy.26 = bf16[16,8,256,128]{3,2,1,0:T(8,128)(2,1)} copy(bf16[16,8,256,128]{2,0,3,1:T(8,128)(2,1)} %bitcast.1) | data formatting | bytes 16777216 | tf_op jit(solution)/shard_map/all_to_all | solution.py:38
  515.8 148.4 %all-to-all-done.2 = bf16[16,1024,256]{2,0,1:T(8,128)(2,1)} async-done(((bf16[16,1024,256]{2,0,1:T(8,128)(2,1)}), bf16[16,1024,256]{2,0,1:T(8,128)(2,1)}, u32[]{:S(2)}, u32[]{:S(2)}) %all-to-all-start.2) | async-done | bytes 8388640 | tf_op jit(solution)/shard_map/all_to_all | solution.py:41
  664.1 11.4 %copy.32 = bf16[16,128,8,256]{3,2,1,0:T(8,128)(2,1)} copy(bf16[16,128,8,256]{3,0,1,2:T(8,128)(2,1)} %bitcast.7) | data formatting | bytes 16777216 | tf_op jit(solution)/shard_map/all_to_all | solution.py:41
  675.5 13.4 %all_to_all.53 = bf16[16,128,2048]{2,1,0:T(8,128)(2,1)} reshape(bf16[16,128,8,256]{3,2,1,0:T(8,128)(2,1)} %copy.32) | data formatting | bytes 16777216 | tf_op jit(solution)/shard_map/all_to_all | solution.py:41
  688.9 0.7 copy.42
  (4 shorter events, 0.1 us)
Async XLA Ops:
  7.2 79.7 %all-reduce.3.cloned.1.call-start = ((), (), s32[]{:S(2)}) async-start(), calls=%async_computation.4 | async-start | bytes 393216 | tf_op jit(solution)/shard_map/psum | solution.py:21
  15.8 12.6 %copy-start.2 = (f32[256,16]{0,1:T(8,128)S(1)}, f32[256,16]{0,1:T(8,128)}, u32[]{:S(2)}) copy-start(f32[256,16]{0,1:T(8,128)} %param.8) | copy-start | bytes 49156
  15.8 12.6 %copy-start.3 = (f32[256]{0:T(256)S(1)}, f32[256]{0:T(256)}, u32[]{:S(2)}) copy-start(f32[256]{0:T(256)} %param.9) | copy-start | bytes 3076
  29.1 68.5 %all-to-all-start.3 = ((bf16[8,256,16]{1,2,0:T(8,128)(2,1)}), bf16[8,256,16]{1,2,0:T(8,128)(2,1)S(1)}, u32[]{:S(2)}, u32[]{:S(2)}) async-start(bf16[8,256,16]{1,2,0:T(8,128)(2,1)} %stack.2), calls=%async_computation.3 | async-start | bytes 131072 | tf_op jit(solution)/shard_map/all_to_all | solution.py:11
  97.6 188.8 %all-to-all-start.1 = ((bf16[16,256,1024]{1,0,2:T(8,128)(2,1)}), bf16[16,256,1024]{1,0,2:T(8,128)(2,1)}, u32[]{:S(2)}, u32[]{:S(2)}) async-start(bf16[16,256,1024]{1,0,2:T(8,128)(2,1)} %divide_convert_fusion), calls=%async_computation.1 | async-start | bytes 16777216 | tf_op jit(solution)/shard_map/all_to_all | solution.py:39
  102.6 17.6 %copy-start.1 = (f32[16,1024]{1,0:T(8,128)S(1)}, f32[16,1024]{1,0:T(8,128)}, u32[]{:S(2)}) copy-start(f32[16,1024]{1,0:T(8,128)} %get-tuple-element.7) | copy-start | bytes 196612
  120.4 171.0 %copy-start = (f32[16,1024]{1,0:T(8,128)S(1)}, f32[16,1024]{1,0:T(8,128)}, u32[]{:S(2)}) copy-start(f32[16,1024]{1,0:T(8,128)} %get-tuple-element.9) | copy-start | bytes 196612
  286.4 188.8 %all-to-all-start = ((bf16[16,256,1024]{1,0,2:T(8,128)(2,1)}), bf16[16,256,1024]{1,0,2:T(8,128)(2,1)}, u32[]{:S(2)}, u32[]{:S(2)}) async-start(bf16[16,256,1024]{1,0,2:T(8,128)(2,1)} %divide_convert_fusion.1), calls=%async_computation | async-start | bytes 16777216 | tf_op jit(solution)/shard_map/all_to_all | solution.py:38
  475.3 188.9 %all-to-all-start.2 = ((bf16[16,1024,256]{2,0,1:T(8,128)(2,1)}), bf16[16,1024,256]{2,0,1:T(8,128)(2,1)}, u32[]{:S(2)}, u32[]{:S(2)}) async-start(bf16[16,1024,256]{2,0,1:T(8,128)(2,1)} %fusion), calls=%async_computation.2 | async-start | bytes 16777216 | tf_op jit(solution)/shard_map/all_to_all | solution.py:41
Sparse Core Ops, SparseCore 0:
  28.6 58.2 all-reduce.2
